TPU v7x, 256 devices: a whole 4x4x8 slice. The times are simulated.
256 devices in a mesh: grp: 16 (over y, x), ep: 16 (over z, core).
Axes of the slice: x: 4, y: 4, z: 8, core: 2. Of those that a mesh axis runs over, the one named last changes fastest.
Arguments:
- tokens: bfloat16 [24576, 4096], P(('grp', 'ep')), may hold values from -6 to 6
- hash_expert: int32 [24576, 1], P(('grp', 'ep')), may hold values from 0 to 15, as said below
- gate_weight: bfloat16 [16, 4096, 4096], P('ep', None, 'grp'), may hold values from -0.09375 to 0.09375
- up_weight: bfloat16 [16, 4096, 4096], P('ep', None, 'grp'), may hold values from -0.09375 to 0.09375
- down_weight: bfloat16 [16, 4096, 4096], P('ep', 'grp'), may hold values from -0.09375 to 0.09375
Outputs:
- combined: bfloat16 [24576, 4096], P(('grp', 'ep'))
- expert_load: float32 [16], replicated
- balance: float32 [], replicated
Inputs may be any that keep to these rules, and one draw needn't show every extreme that they name: `hash_expert`: among the 96 rows of one device no expert is named more than 9 times; on every device some expert is named exactly 9 times; every expert is named by some row.
All inputs are finite; a program needn't handle non-finite values.
Results may differ from a plain program's by a relative error of at most 0.014.
Values may be sent and summed in bfloat16 or wider, within the bound.
A program may use at most 128 MiB of HBM per device.

v0:
```python
import jax
import jax.numpy as jnp
from jax import lax
from jax.sharding import Mesh
from jax.sharding import PartitionSpec as P

EP = ("ep_0", "ep_1")
GRP = ("grp_0", "grp_1")
GRP_EP = ("grp_0", "grp_1", "ep_0", "ep_1")


eps = 1e-06


def one_axis_at_a_time(array, axes):
    for axis in axes:
        array = lax.psum(array, axis)
    return array


def body(tokens, hash_expert, gate_weight, up_weight, down_weight):
    tok_dev, model_width = tokens.shape
    local_experts = gate_weight.shape[0]
    ep_size = lax.axis_size(EP)
    grp_size = lax.axis_size(GRP)
    experts = local_experts * ep_size
    capacity = max(2, 3 * tok_dev // (2 * experts))
    raw_values = tokens.astype(jnp.float32)
    normed = (
        raw_values * lax.rsqrt(jnp.mean(raw_values * raw_values, axis=-1, keepdims=True) + eps)
    ).astype(jnp.bfloat16)
    expert = hash_expert[:, 0]
    onehot = expert[:, None] == jnp.arange(experts, dtype=jnp.int32)[None, :]
    onehot_int = onehot.astype(jnp.int32)
    slot_index = jnp.sum((jnp.cumsum(onehot_int, axis=0) - 1) * onehot_int, axis=1)
    target = expert * capacity + slot_index
    placing = (jnp.arange(experts * capacity, dtype=jnp.int32)[:, None] == target[None, :]).astype(
        jnp.bfloat16
    )
    packed = jnp.dot(placing, normed, preferred_element_type=jnp.float32).astype(jnp.bfloat16)
    packed = packed.reshape(ep_size, local_experts, capacity, model_width)
    received = lax.all_to_all(packed, EP, split_axis=0, concat_axis=0, tiled=True)
    block_rows = lax.all_gather(received, GRP, axis=0, tiled=True)
    gate_out = jnp.einsum(
        "secd,edf->secf", block_rows, gate_weight, preferred_element_type=jnp.float32
    )
    up_out = jnp.einsum("secd,edf->secf", block_rows, up_weight, preferred_element_type=jnp.float32)
    hidden = (jax.nn.silu(gate_out) * up_out).astype(jnp.bfloat16)
    summed = lax.psum_scatter(
        jnp.einsum(
            "secf,efd->secd", hidden, down_weight, preferred_element_type=jnp.float32
        ).astype(jnp.bfloat16),
        GRP,
        scatter_dimension=0,
        tiled=True,
    )
    returned_rows = lax.all_to_all(summed, EP, split_axis=0, concat_axis=1, tiled=True)
    returned = returned_rows.reshape(experts * capacity, model_width)
    combined = jnp.dot(placing.T, returned, preferred_element_type=jnp.float32).astype(jnp.bfloat16)
    counts = one_axis_at_a_time(jnp.sum(onehot.astype(jnp.float32), axis=0), GRP_EP)
    expert_load = counts * experts / (tok_dev * grp_size * ep_size)
    balance = jnp.sum(expert_load * expert_load) / experts
    return (combined, expert_load, balance)


def solution(mesh):
    split = Mesh(mesh.devices.reshape(4, 4, 8, 2), ("grp_0", "grp_1", "ep_0", "ep_1"))
    placed = (
        P(GRP_EP, None),
        P(GRP_EP, None),
        P(EP, None, GRP),
        P(EP, None, GRP),
        P(EP, GRP, None),
    )
    return jax.shard_map(
        body, mesh=split, in_specs=placed, out_specs=(P(GRP_EP, None), P(), P()), check_vma=False
    )
```

profile of v0, /device:TPU:1, one launch (start us, length us, event | category | flops | bytes accessed | tf_op | source)
XLA Modules:
  0.0 449.0 jit_solution(12240543204433801340)
XLA Ops:
  7.2 0.0 copy-start
  7.2 0.0 all-gather.2.cloned.1.call-start
  7.2 0.9 fusion.25
  8.1 0.1 reduce_window_sum.11
  8.2 0.8 select_reduce_fusion
  9.1 0.7 multiply_add_fusion
  9.7 1.4 fusion.11
  11.2 1.7 convolution_convert_fusion
  12.8 1.6 reshape.52
  14.5 60.9 %all_to_all.14 = bf16[16,1,9,4096]{3,2,1,0:T(8,128)(2,1)S(1)} all-to-all(bf16[16,1,9,4096]{3,2,1,0:T(8,128)(2,1)} %bitcast.69), channel_id=1, replica_groups=mesh['grp_0'=4,'grp_1'=4,'ep_0'=8,'ep_1'=2] {'ep_0','ep_1'}, dimensions={0} | all-to-all | bytes 2359296 | tf_op jit(solution)/shard_map/all_to_all | solution.py:42
  75.3 1.8 copy.12
  77.1 0.0 all-gather.2.cloned.1.call-update
  77.1 0.0 reduce-scatter.2.cloned.1.call-start
  77.2 123.7 %all-gather.2.cloned.1.call-done = bf16[256,1,9,4096]{3,0,2,1:T(8,128)(2,1)} async-done(((bf16[16,1,9,4096]{3,0,2,1:T(8,128)(2,1)}), bf16[256,1,9,4096]{3,0,2,1:T(8,128)(2,1)}) %all-gather.2.cloned.1.call-update) | async-done | bytes 18874384 | tf_op jit(solution)/shard_map/all_gather | solution.py:43
  200.8 10.6 %fusion = f32[256,9,256]{2,0,1:T(8,128)} fusion(bf16[256,1,9,4096]{3,0,2,1:T(8,128)(2,1)} %all-gather.2.cloned.1.call-done, bf16[1,4096,256]{2,1,0:T(8,128)(2,1)} %param.8), kind=kOutput, calls=%fused_computation | convolution fusion | flops 4831838208 | bytes 23330816 | tf_op jit(solution)/shard_map/secd,edf->secf/dot_general | solution.py:47
  211.4 0.0 copy-done
  211.4 26.2 %convert_bitcast_fusion = bf16[256,1,9,4096]{3,0,2,1:T(8,128)(2,1)} fusion(bf16[1,256,4096]{2,1,0:T(8,128)(2,1)S(1)} %copy-done, f32[256,9,256]{2,0,1:T(8,128)} %fusion, bf16[256,1,9,4096]{3,0,2,1:T(8,128)(2,1)} %all-gather.2.cloned.1.call-done, bf16[1,4096,256]{2,1,0:T(8,128)(2,1)} %param.7), kind=kOutput, calls=%fused_computation.4 | convolution fusion | flops 9676652544 | bytes 44302336 | tf_op jit(solution)/shard_map/secf,efd->secd/dot_general | solution.py:50
  237.6 0.0 reduce-scatter.2.cloned.1.call-update
  237.6 125.7 %reduce-scatter.2.cloned.1.call-done = bf16[16,1,9,4096]{3,0,2,1:T(8,128)(2,1)} async-done(((bf16[256,1,9,4096]{3,0,2,1:T(8,128)(2,1)}), bf16[16,1,9,4096]{3,0,2,1:T(8,128)(2,1)}) %reduce-scatter.2.cloned.1.call-update) | async-done | bytes 1179664 | tf_op jit(solution)/shard_map/reduce_scatter | solution.py:49
  363.3 3.4 copy.13
  366.7 0.0 copy-start.1
  366.7 8.3 %all-to-all-start.1 = ((bf16[16,1,9,4096]{3,2,1,0:T(8,128)(2,1)}), bf16[16,1,9,4096]{3,2,1,0:T(8,128)(2,1)}, u32[]{:S(2)}, u32[]{:S(2)}) async-start(bf16[16,1,9,4096]{3,2,1,0:T(8,128)(2,1)} %copy.13), calls=%async_computation.2 | async-start | bytes 4194304 | tf_op jit(solution)/shard_map/all_to_all | solution.py:57
  375.0 0.0 copy-done.1
  375.0 0.1 convert_reduce_fusion
  375.1 8.8 %psum.28 = f32[16]{0:T(128)S(1)} all-reduce(f32[16]{0:T(128)S(1)} %convert_reduce_fusion), channel_id=1, replica_groups=mesh['grp_0'=4,'grp_1'=4,'ep_0'=8,'ep_1'=2] {'grp_0'}, use_global_device_ids=true, to_apply=%region_5.6 | all-reduce | flops 16 | bytes 128 | tf_op jit(solution)/shard_map/psum | solution.py:17
  383.9 7.4 %psum.29 = f32[16]{0:T(128)S(1)} all-reduce(f32[16]{0:T(128)S(1)} %psum.28), channel_id=1, replica_groups=mesh['grp_0'=4,'grp_1'=4,'ep_0'=8,'ep_1'=2] {'grp_1'}, use_global_device_ids=true, to_apply=%region_6.7 | all-reduce | flops 16 | bytes 128 | tf_op jit(solution)/shard_map/psum | solution.py:17
  391.3 39.3 %psum.30 = f32[16]{0:T(128)S(1)} all-reduce(f32[16]{0:T(128)S(1)} %psum.29), channel_id=1, replica_groups=mesh['grp_0'=4,'grp_1'=4,'ep_0'=8,'ep_1'=2] {'ep_0'}, use_global_device_ids=true, to_apply=%region_7.8 | all-reduce | flops 16 | bytes 128 | tf_op jit(solution)/shard_map/psum | solution.py:17
  430.6 5.5 %psum.31 = f32[16]{0:T(128)S(1)} all-reduce(f32[16]{0:T(128)S(1)} %psum.30), channel_id=1, replica_groups=mesh['grp_0'=4,'grp_1'=4,'ep_0'=8,'ep_1'=2] {'ep_1'}, use_global_device_ids=true, to_apply=%region_8.9 | all-reduce | flops 16 | bytes 128 | tf_op jit(solution)/shard_map/psum | solution.py:17
  436.1 1.1 multiply_reduce_fusion
  437.9 0.0 all-to-all-done.1
  437.9 1.8 reshape.58
  439.7 1.3 convolution_convert_fusion.1
  (1 shorter events, 0.0 us)
Async XLA Ops:
  7.2 204.3 %copy-start = (bf16[1,256,4096]{2,1,0:T(8,128)(2,1)S(1)}, bf16[1,256,4096]{2,1,0:T(8,128)(2,1)}, u32[]{:S(2)}) copy-start(bf16[1,256,4096]{2,1,0:T(8,128)(2,1)} %param.9) | copy-start | bytes 6291460
  7.2 193.7 %all-gather.2.cloned.1.call-start = ((), (), s32[]{:S(2)}) async-start(), calls=%async_computation.3 | async-start | bytes 20054016 | tf_op jit(solution)/shard_map/all_gather | solution.py:43
  77.1 286.2 %reduce-scatter.2.cloned.1.call-start = ((), (), s32[]{:S(2)}) async-start(), calls=%async_computation.4 | async-start | bytes 20054016 | tf_op jit(solution)/shard_map/reduce_scatter | solution.py:49
  366.7 8.3 %copy-start.1 = (s32[96,1]{0,1:T(1,128)S(1)}, s32[96,1]{0,1:T(1,128)}, u32[]{:S(2)}) copy-start(s32[96,1]{0,1:T(1,128)} %param.6) | copy-start | bytes 1156
  366.7 71.2 %all-to-all-start.1 = ((bf16[16,1,9,4096]{3,2,1,0:T(8,128)(2,1)}), bf16[16,1,9,4096]{3,2,1,0:T(8,128)(2,1)}, u32[]{:S(2)}, u32[]{:S(2)}) async-start(bf16[16,1,9,4096]{3,2,1,0:T(8,128)(2,1)} %copy.13), calls=%async_computation.2 | async-start | bytes 4194304 | tf_op jit(solution)/shard_map/all_to_all | solution.py:57
Sparse Core Ops, SparseCore 0:
  77.2 123.5 all-gather.1
  237.8 125.5 reduce-scatter.1
where the time goes:
time: 449 us
  waiting for transfers between devices  249 us (55%)
  blocking collectives  122 us (27%)
  matrix products  39.8 us (9%)
  between operations  15.9 us (4%)
  local copies, waits for them, and re-layouts  8.61 us (2%)
  starting transfers between devices  8.38 us (2%)
  other arithmetic  5.11 us (1%)
    reduce_scatter x1, waiting for transfers between devices, body(): lax.psum_scatter(jnp.einsum('secf,efd->secd', hidden, down_weight, prefer...  126 us
    all_gather x1, waiting for transfers between devices, body(): block_rows = lax.all_gather(received, GRP, axis=0, tiled=True)  124 us
    psum x4, blocking collectives, one_axis_at_a_time(): array = lax.psum(array, axis)  61 us
    all_to_all x1, blocking collectives, body(): lax.all_to_all(packed, EP, split_axis=0, concat_axis=0, tiled=True)  60.9 us
    dot_general x1, matrix products, body(): jnp.einsum('secf,efd->secd', hidden, down_weight, preferred_element_type=...  26.2 us
    dot_general x1, matrix products, body(): jnp.einsum('secd,edf->secf', block_rows, up_weight, preferred_element_typ...  10.6 us
  transfers between devices with their start and end apart: 3, of which 2 were waited for; matrix products, arithmetic and copies ran while one was open for 0% of the time, Pallas kernels for 0%

commit v1 on v0

v1 whole, which is shorter than its diff:
```python
import functools

import jax
import jax.numpy as jnp
from jax import lax
from jax.experimental import pallas as pl
from jax.experimental.pallas import tpu as pltpu
from jax.sharding import Mesh
from jax.sharding import PartitionSpec as P

EP = ("ep_0", "ep_1")
GRP = ("grp_0", "grp_1")
GRP_EP = ("grp_0", "grp_1", "ep_0", "ep_1")
MESH = pl.DeviceIdType.MESH
CHUNKS = 4

eps = 1e-06


def dot(a, b):
    return jnp.dot(a, b, preferred_element_type=jnp.float32)


def exchange_kernel(
    n_ep,
    packed,
    counts,
    squeeze,
    spread,
    gate,
    up,
    down,
    out,
    totals,
    arrived,
    rows,
    w_in,
    w_out,
    acc,
    hidden,
    far,
    far_in,
    near,
    half_up,
    half_down,
    full_up,
    full_down,
    back,
    count_x,
    count_y,
    count_e,
    z_send,
    z_recv,
    b_send,
    b_recv,
    link_send,
    link_recv,
    w_send,
    w_recv,
    w_local,
    c_send,
    c_recv,
):
    pad, width = packed.shape[1], packed.shape[2]
    own = rows.shape[2]
    units = gate.shape[1]
    cols = width // CHUNKS
    half = cols // 2
    tile = min(256, cols)
    y = lax.axis_index("grp_0")
    x = lax.axis_index("grp_1")
    z = lax.axis_index("ep_0")
    core = lax.axis_index("ep_1")
    me = z * 2 + core
    flip = x + 1 - 2 * (x % 2)
    mirror = 3 - x
    row_mate = mirror + core * (flip - mirror)
    weight_mate = flip + core * (mirror - flip)
    to_rows = {"grp_1": row_mate}
    to_weights = {"grp_1": weight_mate}
    to_up = {"grp_0": (y + 1) % 4}
    to_down = {"grp_0": (y + 3) % 4}

    def ep_peer(d):
        t = (me + d) % n_ep
        return {"ep_0": t // 2, "ep_1": t % 2}

    barrier = pltpu.get_barrier_semaphore()

    def greet(d, carry):
        pl.semaphore_signal(barrier, inc=1, device_id=ep_peer(d), device_id_type=MESH)
        return carry

    lax.fori_loop(1, n_ep, greet, 0)
    for j in range(1, 4):
        pl.semaphore_signal(barrier, inc=1, device_id={"grp_1": (x + j) % 4}, device_id_type=MESH)
        pl.semaphore_signal(barrier, inc=1, device_id={"grp_0": (y + j) % 4}, device_id_type=MESH)
    for r in range(2):
        for c in range(CHUNKS):
            span = pl.ds(c * cols, cols)
            pltpu.make_async_copy(
                (gate, up)[r].at[span, :],
                w_in.at[span, pl.ds(r * units, units)],
                w_local.at[r * CHUNKS + c],
            ).start()
    pltpu.make_async_copy(down, w_out.at[pl.ds(0, units), :], w_local.at[2 * CHUNKS]).start()
    arrived[0] = packed[0]
    count_x[0] = counts[...]
    pl.semaphore_wait(barrier, n_ep - 1 + 6)

    def remote(src, dst, send, recv, device):
        return pltpu.make_async_remote_copy(
            src_ref=src,
            dst_ref=dst,
            send_sem=send,
            recv_sem=recv,
            device_id=device,
            device_id_type=MESH,
        )

    def span_of(c):
        return pl.ds(c * cols, cols)

    def z_copy(c, d, n=None):
        at = d if n is None else pl.ds(d, n)
        return remote(
            packed.at[at, :, span_of(c)],
            arrived.at[at, :, span_of(c)],
            z_send.at[c],
            z_recv.at[c],
            ep_peer(d),
        )

    def back_copy(c, d, n=None):
        at = d if n is None else pl.ds(d, n)
        return remote(
            back.at[at, :, span_of(c)],
            out.at[at, :, span_of(c)],
            b_send.at[c],
            b_recv.at[c],
            ep_peer(n_ep - d),
        )

    def start_all(copy_of, c):
        def go(d, carry):
            copy_of(c, d).start()
            return carry

        lax.fori_loop(1, n_ep, go, 0)

    for c in range(CHUNKS):
        start_all(z_copy, c)

    def weight_copies(c):
        return [
            remote(
                (gate, up)[r].at[span_of(c), :],
                w_in.at[span_of(c), pl.ds((2 + r) * units, units)],
                w_send.at[r * CHUNKS + c],
                w_recv.at[r * CHUNKS + c],
                to_weights,
            )
            for r in range(2)
        ]

    down_copy = remote(
        down,
        w_out.at[pl.ds(units, units), :],
        w_send.at[2 * CHUNKS],
        w_recv.at[2 * CHUNKS],
        to_weights,
    )
    for c in range(CHUNKS):
        for copy in weight_copies(c):
            copy.start()
    down_copy.start()

    def count_copies(buffer, axis, at, sem):
        return [
            remote(buffer.at[0], buffer.at[j], c_send.at[sem], c_recv.at[sem], {axis: (at + j) % 4})
            for j in range(1, 4)
        ]

    def count_all(buffer, n, sem, device):
        return remote(
            buffer.at[pl.ds(1, n)], buffer.at[pl.ds(1, n)], c_send.at[sem], c_recv.at[sem], device
        )

    for copy in count_copies(count_x, "grp_1", x, 0):
        copy.start()

    def link(kind, c, src, dst, device):
        return remote(
            src, dst, link_send.at[kind * CHUNKS + c], link_recv.at[kind * CHUNKS + c], device
        )

    def block(r, k, c):
        return rows.at[r, k, :, span_of(c)]

    def swap_x(c):
        return link(0, c, block(0, 0, c), block(0, 1, c), to_rows)

    def own_up(k, c):
        return link(1 + k, c, block(0, k, c), block(3, k, c), to_up)

    def own_down(k, c):
        return link(3 + k, c, block(0, k, c), block(1, k, c), to_down)

    def pass_up(c):
        return link(5, c, block(3, 0, c), block(2, 0, c), to_up)

    def pass_down(c):
        return link(6, c, block(1, 1, c), block(2, 1, c), to_down)

    def far_copy(c):
        return link(7, c, far.at[:, :, span_of(c)], far_in.at[:, :, span_of(c)], to_rows)

    def half_up_copy(c):
        return link(
            8,
            c,
            near.at[2, :, pl.ds(c * cols, half)],
            half_up.at[:, pl.ds(c * half, half)],
            to_up,
        )

    def half_down_copy(c):
        return link(
            9,
            c,
            near.at[2, :, pl.ds(c * cols + half, half)],
            half_down.at[:, pl.ds(c * half, half)],
            to_down,
        )

    def full_up_copy(c):
        return link(10, c, near.at[1, :, span_of(c)], full_up.at[:, span_of(c)], to_up)

    def full_down_copy(c):
        return link(11, c, near.at[3, :, span_of(c)], full_down.at[:, span_of(c)], to_down)

    def stage_a(c):
        z_copy(c, 1, n_ep - 1).wait_recv()
        span = span_of(c)
        step = min(512, cols)
        for s in range(cols // step):
            part = pl.ds(c * cols + s * step, step)
            rows[0, 0, :, part] = dot(
                squeeze[...], arrived[:, :, part].reshape(n_ep * pad, step)
            ).astype(jnp.bfloat16)
        swap_x(c).start()
        own_up(0, c).start()
        own_down(0, c).start()

    def stage_b(c):
        swap_x(c).wait_recv()
        own_up(1, c).start()
        own_down(1, c).start()

    def stage_c(c):
        own_up(0, c).wait_recv()
        pass_up(c).start()
        own_down(1, c).wait_recv()
        pass_down(c).start()

    def multiply(c, r):
        left = rows[r, :, :, span_of(c)].reshape(2 * own, cols)

        def one(n, carry):
            part = pl.ds(pl.multiple_of(n * units, units), units)
            product = dot(left, w_in[span_of(c), part])
            if c == 0:
                acc[r, :, part] = product
            else:
                acc[r, :, part] += product
            return carry

        lax.fori_loop(0, 4, one, 0)
        if c == CHUNKS - 1:
            for k in range(2):
                g = acc[r, :, pl.ds(2 * k * units, units)]
                u = acc[r, :, pl.ds((2 * k + 1) * units, units)]
                hidden[r, :, pl.ds(k * units, units)] = (jax.nn.silu(g) * u).astype(jnp.bfloat16)

    def stage_d(c):
        for r in range(2):
            pltpu.make_async_copy(
                (gate, up)[r].at[span_of(c), :],
                w_in.at[span_of(c), pl.ds(r * units, units)],
                w_local.at[r * CHUNKS + c],
            ).wait()
        for copy in weight_copies(c):
            copy.wait_recv()
        own_down(0, c).wait_recv()
        own_up(1, c).wait_recv()

        def three(i, carry):
            multiply(c, i + i // 2)
            return carry

        lax.fori_loop(0, 3, three, 0)
        pass_up(c).wait_recv()
        pass_down(c).wait_recv()
        multiply(c, 2)

    def project(c, r, k, s):
        part = pl.ds(pl.multiple_of(c * cols + s * tile, tile), tile)
        return part, dot(hidden[r, pl.ds(k * own, own), :], w_out[:, part])

    def stage_e(c):
        def one(i, carry):
            r, s = i // (cols // tile), i % (cols // tile)
            part, value = project(c, r, 1, s)
            far[r, :, part] = value.astype(jnp.bfloat16)
            return carry

        lax.fori_loop(0, 4 * (cols // tile), one, 0)
        far_copy(c).start()

    def near_sum(c, r):
        def one(s, carry):
            part, value = project(c, r, 0, s)
            near[r, :, part] = (value + far_in[r, :, part].astype(jnp.float32)).astype(jnp.bfloat16)
            return carry

        lax.fori_loop(0, cols // tile, one, 0)

    def stage_f(c):
        far_copy(c).wait_recv()
        near_sum(c, 2)
        half_up_copy(c).start()
        half_down_copy(c).start()

        def three(i, carry):
            near_sum(c, i + i // 2)
            return carry

        lax.fori_loop(0, 3, three, 0)

    def add_into(r, at, other):
        near[r, :, at] = (near[r, :, at].astype(jnp.float32) + other.astype(jnp.float32)).astype(
            jnp.bfloat16
        )

    def stage_g(c):
        half_up_copy(c).wait_recv()
        add_into(1, pl.ds(c * cols, half), half_up[:, pl.ds(c * half, half)])
        full_up_copy(c).start()
        half_down_copy(c).wait_recv()
        add_into(3, pl.ds(c * cols + half, half), half_down[:, pl.ds(c * half, half)])
        full_down_copy(c).start()

    def stage_h(c):
        full_up_copy(c).wait_recv()
        full_down_copy(c).wait_recv()
        for s in range(cols // tile):
            part = pl.ds(c * cols + s * tile, tile)
            total = (
                near[0, :, part].astype(jnp.float32)
                + full_up[:, part].astype(jnp.float32)
                + full_down[:, part].astype(jnp.float32)
            ).astype(jnp.bfloat16)
            back[:, :, part] = (
                dot(spread[...], total).astype(jnp.bfloat16).reshape(n_ep, pad, tile)
            )
        start_all(back_copy, c)
        out[0, :, span_of(c)] = back[0, :, span_of(c)]

    def count_step_x():
        count_all(count_x, 3, 0, to_rows).wait_recv()
        count_y[0] = count_x[0] + count_x[1] + count_x[2] + count_x[3]
        for copy in count_copies(count_y, "grp_0", y, 1):
            copy.start()

    def count_step_y():
        count_all(count_y, 3, 1, to_up).wait_recv()
        count_e[0] = count_y[0] + count_y[1] + count_y[2] + count_y[3]

        def go(d, carry):
            remote(count_e.at[0], count_e.at[d], c_send.at[2], c_recv.at[2], ep_peer(d)).start()
            return carry

        lax.fori_loop(1, n_ep, go, 0)

    for step in range(CHUNKS + 3):
        if step < CHUNKS:
            stage_a(step)
        if step == 0:
            count_step_x()
        if 0 <= step - 1 < CHUNKS:
            stage_c(step - 1)
        if step == 1:
            count_step_y()
        if step < CHUNKS:
            stage_b(step)
        if 0 <= step - 2 < CHUNKS:
            stage_d(step - 2)
    pltpu.make_async_copy(down, w_out.at[pl.ds(0, units), :], w_local.at[2 * CHUNKS]).wait()
    down_copy.wait_recv()
    for c in range(CHUNKS):
        stage_e(c)
    for step in range(CHUNKS + 1):
        if step < CHUNKS:
            stage_f(step)
        if step >= 1:
            stage_h(step - 1)
        if step < CHUNKS:
            stage_g(step)
    count_all(count_e, n_ep - 1, 2, ep_peer(1)).wait_recv()
    totals[...] = jnp.sum(count_e[...], axis=0)
    for c in range(CHUNKS):
        z_copy(c, 1, n_ep - 1).wait_send()
        for copy in weight_copies(c):
            copy.wait_send()
        for copy in (
            swap_x(c),
            own_up(0, c),
            own_up(1, c),
            own_down(0, c),
            own_down(1, c),
            pass_up(c),
            pass_down(c),
            far_copy(c),
            half_up_copy(c),
            half_down_copy(c),
            full_up_copy(c),
            full_down_copy(c),
        ):
            copy.wait_send()
    down_copy.wait_send()
    count_all(count_x, 3, 0, to_rows).wait_send()
    count_all(count_y, 3, 1, to_up).wait_send()
    count_all(count_e, n_ep - 1, 2, ep_peer(1)).wait_send()
    for c in range(CHUNKS):
        back_copy(c, 1, n_ep - 1).wait_recv()
        back_copy(c, 1, n_ep - 1).wait_send()


def exchange(packed, counts, squeeze, spread, gate, up, down):
    n_ep, pad, width = packed.shape
    own = squeeze.shape[0]
    units = gate.shape[1]
    half = width // 2
    bf16, f32 = jnp.bfloat16, jnp.float32
    vmem = pl.BlockSpec(memory_space=pltpu.VMEM)
    hbm = pl.BlockSpec(memory_space=pl.ANY)
    dma = pltpu.SemaphoreType.DMA
    return pl.pallas_call(
        functools.partial(exchange_kernel, n_ep),
        out_shape=(
            jax.ShapeDtypeStruct((n_ep, pad, width), bf16),
            jax.ShapeDtypeStruct(counts.shape, f32),
        ),
        in_specs=[vmem, vmem, vmem, vmem, hbm, hbm, hbm],
        out_specs=(vmem, vmem),
        scratch_shapes=[
            pltpu.VMEM((n_ep, pad, width), bf16),
            pltpu.VMEM((4, 2, own, width), bf16),
            pltpu.VMEM((width, 4 * units), bf16),
            pltpu.VMEM((2 * units, width), bf16),
            pltpu.VMEM((4, 2 * own, 4 * units), f32),
            pltpu.VMEM((4, 2 * own, 2 * units), bf16),
            pltpu.VMEM((4, own, width), bf16),
            pltpu.VMEM((4, own, width), bf16),
            pltpu.VMEM((4, own, width), bf16),
            pltpu.VMEM((own, half), bf16),
            pltpu.VMEM((own, half), bf16),
            pltpu.VMEM((own, width), bf16),
            pltpu.VMEM((own, width), bf16),
            pltpu.VMEM((n_ep, pad, width), bf16),
            pltpu.VMEM((4,) + counts.shape, f32),
            pltpu.VMEM((4,) + counts.shape, f32),
            pltpu.VMEM((n_ep,) + counts.shape, f32),
            dma((CHUNKS,)),
            dma((CHUNKS,)),
            dma((CHUNKS,)),
            dma((CHUNKS,)),
            dma((12 * CHUNKS,)),
            dma((12 * CHUNKS,)),
            dma((2 * CHUNKS + 1,)),
            dma((2 * CHUNKS + 1,)),
            dma((2 * CHUNKS + 1,)),
            dma((3,)),
            dma((3,)),
        ],
        compiler_params=pltpu.CompilerParams(
            collective_id=0, has_side_effects=True, vmem_limit_bytes=67_000_000
        ),
    )(packed, counts, squeeze, spread, gate, up, down)


def body(tokens, hash_expert, gate_weight, up_weight, down_weight):
    tok_dev, model_width = tokens.shape
    ep_size = lax.axis_size(EP)
    grp_size = lax.axis_size(GRP)
    experts = gate_weight.shape[0] * ep_size
    capacity = max(2, 3 * tok_dev // (2 * experts))
    pad = -(-capacity // 16) * 16
    raw_values = tokens.astype(jnp.float32)
    normed = (
        raw_values * lax.rsqrt(jnp.mean(raw_values * raw_values, axis=-1, keepdims=True) + eps)
    ).astype(jnp.bfloat16)
    expert = hash_expert[:, 0]
    onehot = expert[:, None] == jnp.arange(experts, dtype=jnp.int32)[None, :]
    onehot_int = onehot.astype(jnp.int32)
    slot_index = jnp.sum((jnp.cumsum(onehot_int, axis=0) - 1) * onehot_int, axis=1)
    me = lax.axis_index("ep_0") * 2 + lax.axis_index("ep_1")
    target = ((expert - me + experts) % experts) * pad + slot_index
    placing = (jnp.arange(experts * pad, dtype=jnp.int32)[:, None] == target[None, :]).astype(
        jnp.bfloat16
    )
    packed = jnp.dot(placing, normed, preferred_element_type=jnp.float32).astype(jnp.bfloat16)
    packed = packed.reshape(experts, pad, model_width)
    place = jnp.arange(experts * capacity, dtype=jnp.int32)
    place = (place // capacity) * pad + place % capacity
    squeeze = place[:, None] == jnp.arange(experts * pad, dtype=jnp.int32)[None, :]
    counts = jnp.sum(onehot.astype(jnp.float32), axis=0)
    counts = jnp.pad(counts[None, :], ((0, 7), (0, 128 - experts)))
    returned, totals = exchange(
        packed,
        counts,
        squeeze.astype(jnp.bfloat16),
        squeeze.T.astype(jnp.bfloat16),
        gate_weight[0],
        up_weight[0],
        down_weight[0],
    )
    returned = returned.reshape(experts * pad, model_width)
    combined = jnp.dot(placing.T, returned, preferred_element_type=jnp.float32).astype(jnp.bfloat16)
    expert_load = totals[0, :experts] * experts / (tok_dev * grp_size * ep_size)
    balance = jnp.sum(expert_load * expert_load) / experts
    return (combined, expert_load, balance)


def solution(mesh):
    grp, ep = mesh.devices.shape
    split = Mesh(mesh.devices.reshape(4, 4, ep // 2, 2), GRP_EP)
    placed = (
        P(GRP_EP, None),
        P(GRP_EP, None),
        P(EP, None, GRP),
        P(EP, None, GRP),
        P(EP, GRP, None),
    )
    return jax.shard_map(
        body, mesh=split, in_specs=placed, out_specs=(P(GRP_EP, None), P(), P()), check_vma=False
    )
```

time: 449 us -> 263 us (0.59)
  waiting for transfers between devices: 249 us -> 0 us
  Pallas kernels: 0 us -> 246 us
  blocking collectives: 122 us -> 0 us
  matrix products: 39.8 us -> 6.25 us
  between operations: 15.9 us -> 2.45 us
  starting transfers between devices: 8.38 us -> 0 us
  local copies, waits for them, and re-layouts: 8.61 us -> 0.6 us
    pallas_call x0 -> x1, Pallas kernels: none -> 246 us  [exchange(): pl.pallas_call(functools.partial(exchange_kernel, n_ep), out_shape=(jax.S...]
    reduce_scatter x1 -> x0, waiting for transfers between devices: 126 us -> none  [body(): lax.psum_scatter(jnp.einsum('secf,efd->secd', hidden, down_weight, prefer...]
    all_gather x1 -> x0, waiting for transfers between devices: 124 us -> none  [body(): block_rows = lax.all_gather(received, GRP, axis=0, tiled=True)]
    psum x4 -> x0, blocking collectives: 61 us -> none  [one_axis_at_a_time(): array = lax.psum(array, axis)]
    all_to_all x1 -> x0, blocking collectives: 60.9 us -> none  [body(): lax.all_to_all(packed, EP, split_axis=0, concat_axis=0, tiled=True)]
    dot_general x2 -> x0, matrix products: 36.8 us -> none  [the longest x1 26.2 us: body(): jnp.einsum('secf,efd->secd', hidden, down_weight, preferred_element_type=...]
    all_to_all x1 -> x0, starting transfers between devices: 8.3 us -> none  [body(): lax.all_to_all(summed, EP, split_axis=0, concat_axis=1, tiled=True)]
  transfers between devices with their start and end apart: 3 -> 0, of which waited for: 2 -> 0; matrix products, arithmetic and copies ran while one was open for 0% -> 0% of each run, Pallas kernels for 0% -> 0%
where the time goes in v1:
time: 263 us
  Pallas kernels  246 us (94%)
  other arithmetic  7.73 us (3%)
  matrix products  6.25 us (2%)
    pallas_call x1, Pallas kernels, exchange(): pl.pallas_call(functools.partial(exchange_kernel, n_ep), out_shape=(jax.S...  246 us

profile of v1, /device:TPU:1, one launch (start us, length us, event | category | flops | bytes accessed | tf_op | source)
XLA Modules:
  0.0 262.6 jit_solution(4474518965657427033)
XLA Ops:
  0.6 1.4 fusion
  2.0 0.8 convert_reduce_fusion
  2.8 0.6 pad.4.counts
  3.4 0.7 fusion.8
  4.2 0.1 reduce_window_sum.11
  4.3 0.8 select_reduce_fusion
  5.1 0.7 fusion.14
  5.8 0.7 fusion.5.squeeze
  6.5 0.7 fusion.4.spread
  7.2 3.3 %convolution_convert_fusion = bf16[256,4096]{1,0:T(8,128)(2,1)} fusion(bf16[96,4096]{1,0:T(8,128)(2,1)} %param.5, f32[96]{0:T(128)S(1)} %add_rsqrt_fusion, s32[96]{0:T(128)S(1)} %fusion.14), kind=kOutput, calls=%fused_computation | convolution fusion | flops 203579392 | bytes 2884352 | tf_op jit(solution)/shard_map/dot_general | solution.py:512
  10.5 245.6 %shard_map.76 = (bf16[16,16,4096]{2,1,0:T(8,128)(2,1)}, f32[8,128]{1,0:T(8,128)}) custom-call(bf16[16,16,4096]{2,1,0:T(8,128)(2,1)} %bitcast.12, f32[8,128]{1,0:T(8,128)} %pad.4.counts, bf16[144,256]{1,0:T(8,128)(2,1)} %fusion.5.squeeze, bf16[256,144]{1,0:T(8,128)(2,1)} %fusion.4.spread, bf16[4096,256]{1,0:T(8,128)(2,1)} %bitcast.13, ...), custom_call_target="tpu_custom_call" | custom-call | tf_op jit(solution)/shard_map/pallas_call | solution.py:448
  256.1 3.0 %convolution_convert_fusion.1 = bf16[96,4096]{1,0:T(8,128)(2,1)} fusion(bf16[256,4096]{1,0:T(8,128)(2,1)} %bitcast.16, s32[96]{0:T(128)S(1)} %fusion.14), kind=kOutput, calls=%fused_computation.1 | convolution fusion | flops 201744384 | bytes 2883968 | tf_op jit(solution)/shard_map/dot_general | solution.py:529
  259.1 1.8 multiply_reduce_fusion
  (2 shorter events, 0.0 us)

commit v2 on v1

--- a/solution.py
+++ b/solution.py
@@ -2,6 +2,7 @@
 
 import jax
 import jax.numpy as jnp
+import numpy as np
 from jax import lax
 from jax.experimental import pallas as pl
 from jax.experimental.pallas import tpu as pltpu
@@ -12,7 +13,7 @@
 GRP = ("grp_0", "grp_1")
 GRP_EP = ("grp_0", "grp_1", "ep_0", "ep_1")
 MESH = pl.DeviceIdType.MESH
-CHUNKS = 4
+CHUNKS = 8
 
 eps = 1e-06
 
@@ -23,15 +24,20 @@
 
 def exchange_kernel(
     n_ep,
-    packed,
-    counts,
+    capacity,
+    tokens,
+    experts_of,
     squeeze,
     spread,
     gate,
     up,
     down,
     out,
-    totals,
+    load,
+    balance,
+    packed,
+    collect,
+    returned,
     arrived,
     rows,
     w_in,
@@ -104,8 +110,43 @@
                 w_local.at[r * CHUNKS + c],
             ).start()
     pltpu.make_async_copy(down, w_out.at[pl.ds(0, units), :], w_local.at[2 * CHUNKS]).start()
+
+    n_tok = tokens.shape[0]
+    f32, bf16 = jnp.float32, jnp.bfloat16
+    named = experts_of[...]
+    picks = (lax.broadcasted_iota(jnp.int32, (n_ep, n_tok), 0) == named).astype(f32)
+    before = lax.broadcasted_iota(jnp.int32, (n_tok, n_tok), 0) < lax.broadcasted_iota(
+        jnp.int32, (n_tok, n_tok), 1
+    )
+    earlier = dot(picks.astype(bf16), before.astype(bf16))
+    slot = jnp.sum(earlier * picks, axis=0, keepdims=True).astype(jnp.int32)
+    away = named - me
+    away = jnp.where(away < 0, away + n_ep, away)
+    target = away * pad + slot
+    placing = (
+        lax.broadcasted_iota(jnp.int32, (n_ep * pad, n_tok), 0) == target
+    ).astype(f32).astype(bf16)
+    same = lax.broadcasted_iota(jnp.int32, (n_tok, n_tok), 0) == lax.broadcasted_iota(
+        jnp.int32, (n_tok, n_tok), 1
+    )
+    target_down = jnp.sum(jnp.where(same, target.astype(f32), 0.0), axis=1, keepdims=True).astype(
+        jnp.int32
+    )
+    collect[...] = (
+        lax.broadcasted_iota(jnp.int32, (n_tok, n_ep * pad), 1) == target_down
+    ).astype(f32).astype(bf16)
+    count_x[0] = jnp.broadcast_to(jnp.sum(picks, axis=1, keepdims=True), count_x.shape[1:])
+    step = min(512, width)
+    squares = jnp.zeros((n_tok, 1), f32)
+    for s in range(width // step):
+        value = tokens[:, pl.ds(s * step, step)].astype(f32)
+        squares += jnp.sum(value * value, axis=1, keepdims=True)
+    scale = lax.rsqrt(squares / width + eps)
+    for s in range(width // step):
+        part = pl.ds(s * step, step)
+        normed = (tokens[:, part].astype(f32) * scale).astype(bf16)
+        packed[:, :, part] = dot(placing, normed).astype(bf16).reshape(n_ep, pad, step)
     arrived[0] = packed[0]
-    count_x[0] = counts[...]
     pl.semaphore_wait(barrier, n_ep - 1 + 6)
 
     def remote(src, dst, send, recv, device):
@@ -135,7 +176,7 @@
         at = d if n is None else pl.ds(d, n)
         return remote(
             back.at[at, :, span_of(c)],
-            out.at[at, :, span_of(c)],
+            returned.at[at, :, span_of(c)],
             b_send.at[c],
             b_recv.at[c],
             ep_peer(n_ep - d),
@@ -147,9 +188,6 @@
             return carry
 
         lax.fori_loop(1, n_ep, go, 0)
-
-    for c in range(CHUNKS):
-        start_all(z_copy, c)
 
     def weight_copies(c):
         return [
@@ -163,17 +201,14 @@
             for r in range(2)
         ]
 
-    down_copy = remote(
-        down,
-        w_out.at[pl.ds(units, units), :],
-        w_send.at[2 * CHUNKS],
-        w_recv.at[2 * CHUNKS],
-        to_weights,
-    )
-    for c in range(CHUNKS):
-        for copy in weight_copies(c):
-            copy.start()
-    down_copy.start()
+    def down_copy(c):
+        return remote(
+            down.at[:, span_of(c)],
+            w_out.at[pl.ds(units, units), span_of(c)],
+            w_send.at[2 * CHUNKS + c],
+            w_recv.at[2 * CHUNKS + c],
+            to_weights,
+        )
 
     def count_copies(buffer, axis, at, sem):
         return [
@@ -364,7 +399,12 @@
                 dot(spread[...], total).astype(jnp.bfloat16).reshape(n_ep, pad, tile)
             )
         start_all(back_copy, c)
-        out[0, :, span_of(c)] = back[0, :, span_of(c)]
+        returned[0, :, span_of(c)] = back[0, :, span_of(c)]
+
+    def stage_i(c):
+        back_copy(c, 1, n_ep - 1).wait_recv()
+        block_rows = returned[:, :, span_of(c)].reshape(n_ep * pad, cols)
+        out[:, span_of(c)] = dot(collect[...], block_rows).astype(bf16)
 
     def count_step_x():
         count_all(count_x, 3, 0, to_rows).wait_recv()
@@ -382,9 +422,15 @@
 
         lax.fori_loop(1, n_ep, go, 0)
 
-    for step in range(CHUNKS + 3):
+    start_all(z_copy, 0)
+    for copy in weight_copies(0):
+        copy.start()
+    start_all(z_copy, 1)
+    for step in range(CHUNKS + 2):
         if step < CHUNKS:
             stage_a(step)
+        if step + 2 < CHUNKS:
+            start_all(z_copy, step + 2)
         if step == 0:
             count_step_x()
         if 0 <= step - 1 < CHUNKS:
@@ -393,25 +439,41 @@
             count_step_y()
         if step < CHUNKS:
             stage_b(step)
+        if step + 1 < CHUNKS:
+            for copy in weight_copies(step + 1):
+                copy.start()
+        if step < CHUNKS:
+            down_copy(step).start()
         if 0 <= step - 2 < CHUNKS:
             stage_d(step - 2)
     pltpu.make_async_copy(down, w_out.at[pl.ds(0, units), :], w_local.at[2 * CHUNKS]).wait()
-    down_copy.wait_recv()
     for c in range(CHUNKS):
-        stage_e(c)
-    for step in range(CHUNKS + 1):
+        down_copy(c).wait_recv()
+    stage_e(0)
+    stage_e(1)
+    for step in range(CHUNKS + 3):
         if step < CHUNKS:
             stage_f(step)
-        if step >= 1:
+        if step + 2 < CHUNKS:
+            stage_e(step + 2)
+        if 1 <= step <= CHUNKS:
             stage_h(step - 1)
         if step < CHUNKS:
             stage_g(step)
+        if step >= 3:
+            stage_i(step - 3)
     count_all(count_e, n_ep - 1, 2, ep_peer(1)).wait_recv()
-    totals[...] = jnp.sum(count_e[...], axis=0)
+    share = jnp.sum(count_e[...], axis=0) * n_ep / (n_tok * 16 * n_ep)
+    at_lane = lax.broadcasted_iota(jnp.int32, share.shape, 0) == lax.broadcasted_iota(
+        jnp.int32, share.shape, 1
+    )
+    load[...] = jnp.sum(jnp.where(at_lane, share, 0.0), axis=0, keepdims=True)
+    balance[...] = jnp.sum(share * share, axis=0, keepdims=True) / n_ep
     for c in range(CHUNKS):
         z_copy(c, 1, n_ep - 1).wait_send()
         for copy in weight_copies(c):
             copy.wait_send()
+        down_copy(c).wait_send()
         for copy in (
             swap_x(c),
             own_up(0, c),
@@ -427,33 +489,41 @@
             full_down_copy(c),
         ):
             copy.wait_send()
-    down_copy.wait_send()
     count_all(count_x, 3, 0, to_rows).wait_send()
     count_all(count_y, 3, 1, to_up).wait_send()
     count_all(count_e, n_ep - 1, 2, ep_peer(1)).wait_send()
     for c in range(CHUNKS):
-        back_copy(c, 1, n_ep - 1).wait_recv()
         back_copy(c, 1, n_ep - 1).wait_send()
 
 
-def exchange(packed, counts, squeeze, spread, gate, up, down):
-    n_ep, pad, width = packed.shape
-    own = squeeze.shape[0]
-    units = gate.shape[1]
+def body(tokens, hash_expert, gate_weight, up_weight, down_weight):
+    n_tok, width = tokens.shape
+    n_ep = lax.axis_size(EP)
+    units = gate_weight.shape[2]
+    capacity = max(2, 3 * n_tok // (2 * n_ep))
+    pad = -(-capacity // 16) * 16
+    own = n_ep * capacity
     half = width // 2
+    place = np.arange(own)
+    place = (place // capacity) * pad + place % capacity
+    squeeze = place[:, None] == np.arange(n_ep * pad)[None, :]
     bf16, f32 = jnp.bfloat16, jnp.float32
     vmem = pl.BlockSpec(memory_space=pltpu.VMEM)
     hbm = pl.BlockSpec(memory_space=pl.ANY)
     dma = pltpu.SemaphoreType.DMA
-    return pl.pallas_call(
-        functools.partial(exchange_kernel, n_ep),
+    combined, load, balance = pl.pallas_call(
+        functools.partial(exchange_kernel, n_ep, capacity),
         out_shape=(
-            jax.ShapeDtypeStruct((n_ep, pad, width), bf16),
-            jax.ShapeDtypeStruct(counts.shape, f32),
+            jax.ShapeDtypeStruct((n_tok, width), bf16),
+            jax.ShapeDtypeStruct((1, 128), f32),
+            jax.ShapeDtypeStruct((1, 128), f32),
         ),
         in_specs=[vmem, vmem, vmem, vmem, hbm, hbm, hbm],
-        out_specs=(vmem, vmem),
+        out_specs=(vmem, vmem, vmem),
         scratch_shapes=[
+            pltpu.VMEM((n_ep, pad, width), bf16),
+            pltpu.VMEM((n_tok, n_ep * pad), bf16),
+            pltpu.VMEM((n_ep, pad, width), bf16),
             pltpu.VMEM((n_ep, pad, width), bf16),
             pltpu.VMEM((4, 2, own, width), bf16),
             pltpu.VMEM((width, 4 * units), bf16),
@@ -468,17 +538,17 @@
             pltpu.VMEM((own, width), bf16),
             pltpu.VMEM((own, width), bf16),
             pltpu.VMEM((n_ep, pad, width), bf16),
-            pltpu.VMEM((4,) + counts.shape, f32),
-            pltpu.VMEM((4,) + counts.shape, f32),
-            pltpu.VMEM((n_ep,) + counts.shape, f32),
+            pltpu.VMEM((4, n_ep, 128), f32),
+            pltpu.VMEM((4, n_ep, 128), f32),
+            pltpu.VMEM((n_ep, n_ep, 128), f32),
             dma((CHUNKS,)),
             dma((CHUNKS,)),
             dma((CHUNKS,)),
             dma((CHUNKS,)),
             dma((12 * CHUNKS,)),
             dma((12 * CHUNKS,)),
-            dma((2 * CHUNKS + 1,)),
-            dma((2 * CHUNKS + 1,)),
+            dma((3 * CHUNKS,)),
+            dma((3 * CHUNKS,)),
             dma((2 * CHUNKS + 1,)),
             dma((3,)),
             dma((3,)),
@@ -486,50 +556,16 @@
         compiler_params=pltpu.CompilerParams(
             collective_id=0, has_side_effects=True, vmem_limit_bytes=67_000_000
         ),
-    )(packed, counts, squeeze, spread, gate, up, down)
-
-
-def body(tokens, hash_expert, gate_weight, up_weight, down_weight):
-    tok_dev, model_width = tokens.shape
-    ep_size = lax.axis_size(EP)
-    grp_size = lax.axis_size(GRP)
-    experts = gate_weight.shape[0] * ep_size
-    capacity = max(2, 3 * tok_dev // (2 * experts))
-    pad = -(-capacity // 16) * 16
-    raw_values = tokens.astype(jnp.float32)
-    normed = (
-        raw_values * lax.rsqrt(jnp.mean(raw_values * raw_values, axis=-1, keepdims=True) + eps)
-    ).astype(jnp.bfloat16)
-    expert = hash_expert[:, 0]
-    onehot = expert[:, None] == jnp.arange(experts, dtype=jnp.int32)[None, :]
-    onehot_int = onehot.astype(jnp.int32)
-    slot_index = jnp.sum((jnp.cumsum(onehot_int, axis=0) - 1) * onehot_int, axis=1)
-    me = lax.axis_index("ep_0") * 2 + lax.axis_index("ep_1")
-    target = ((expert - me + experts) % experts) * pad + slot_index
-    placing = (jnp.arange(experts * pad, dtype=jnp.int32)[:, None] == target[None, :]).astype(
-        jnp.bfloat16
-    )
-    packed = jnp.dot(placing, normed, preferred_element_type=jnp.float32).astype(jnp.bfloat16)
-    packed = packed.reshape(experts, pad, model_width)
-    place = jnp.arange(experts * capacity, dtype=jnp.int32)
-    place = (place // capacity) * pad + place % capacity
-    squeeze = place[:, None] == jnp.arange(experts * pad, dtype=jnp.int32)[None, :]
-    counts = jnp.sum(onehot.astype(jnp.float32), axis=0)
-    counts = jnp.pad(counts[None, :], ((0, 7), (0, 128 - experts)))
-    returned, totals = exchange(
-        packed,
-        counts,
-        squeeze.astype(jnp.bfloat16),
-        squeeze.T.astype(jnp.bfloat16),
+    )(
+        tokens,
+        hash_expert.reshape(1, n_tok),
+        jnp.asarray(squeeze, dtype=bf16),
+        jnp.asarray(squeeze.T, dtype=bf16),
         gate_weight[0],
         up_weight[0],
         down_weight[0],
     )
-    returned = returned.reshape(experts * pad, model_width)
-    combined = jnp.dot(placing.T, returned, preferred_element_type=jnp.float32).astype(jnp.bfloat16)
-    expert_load = totals[0, :experts] * experts / (tok_dev * grp_size * ep_size)
-    balance = jnp.sum(expert_load * expert_load) / experts
-    return (combined, expert_load, balance)
+    return (combined, load[0, :n_ep], balance[0, 0])
 
 
 def solution(mesh):

time: 263 us -> 189 us (0.72)
  Pallas kernels: 246 us -> 184 us
  other arithmetic: 7.73 us -> 0 us
  matrix products: 6.25 us -> 0 us
    pallas_call x1, Pallas kernels: 246 us -> 184 us  [body(): pl.pallas_call(functools.partial(exchange_kernel, n_ep, capacity), out_sh...]
    dot_general x2 -> x0, matrix products: 6.25 us -> none  [the longest x1 3.26 us: body(): jnp.dot(placing, normed, preferred_element_type=jnp.float32)]
    reduce_sum x4 -> x0, other arithmetic: 4.76 us -> none  [the longest x1 1.78 us: body(): balance = jnp.sum(expert_load * expert_load) / experts]
where the time goes in v2:
time: 189 us
  Pallas kernels  184 us (97%)
  local copies, waits for them, and re-layouts  3.15 us (2%)
  between operations  2.41 us (1%)
    pallas_call x1, Pallas kernels, body(): pl.pallas_call(functools.partial(exchange_kernel, n_ep, capacity), out_sh...  184 us

profile of v2, /device:TPU:1, one launch (start us, length us, event | category | flops | bytes accessed | tf_op | source)
XLA Modules:
  0.0 189.1 jit_solution(15489945750289352270)
XLA Ops:
  0.6 183.6 %shard_map.94 = (bf16[96,4096]{1,0:T(8,128)(2,1)}, f32[1,128]{1,0:T(1,128)}, f32[1,128]{1,0:T(1,128)}) custom-call(bf16[96,4096]{1,0:T(8,128)(2,1)} %tokens.1, s32[1,96]{1,0:T(1,128)} %bitcast.11, bf16[144,256]{1,0:T(8,128)(2,1)} %constant.4.clone.squeeze, bf16[256,144]{1,0:T(8,128)(2,1)} %constant.5.clone.spread, bf16[4096,256]{1,0:T(8,128)(2,1)} %bitcast.8, ...), custom_call_target="tpu_custom_call" | custom-call | tf_op jit(solution)/shard_map/pallas_call | solution.py:514
  184.2 1.1 slice_bitcast_fusion
  185.3 2.1 %copy.12 = bf16[96,4096]{1,0:T(8,128)(2,1)} copy(bf16[96,4096]{1,0:T(8,128)(2,1)} %get-tuple-element.12) | data formatting | bytes 1572864
